TPU v7x, 32 devices: a whole 2x2x4 slice. The times are simulated.
32 devices in a mesh: rows: 4 (over z), cx: 2 (over y), cy: 4 (over x, core).
Axes of the slice: x: 2, y: 2, z: 4, core: 2. Of those that a mesh axis runs over, the one named last changes fastest.
Arguments:
- rows_data: float32 [2048, 1024], P(('rows', 'cx', 'cy')), may hold values from -6 to 6
- owner_rows: int32 [2048, 1], P(('rows', 'cx', 'cy')), may hold values from 0 to 7; in each aligned block of 64 rows (0 to 63, 64 to 127, ...) at most 16 rows name the same one
- slot_rows: int32 [2048], P(('rows', 'cx', 'cy')), may hold values from 0 to 2047
- centroids: float32 [16384, 1024], P(('cx', 'cy'), 'rows'), may hold values from -6 to 6
- counts: float32 [16384], P(('cx', 'cy')), may hold values from 1 to 100
- owner_cent: int32 [16384, 1], P(('cx', 'cy')), may hold values from 0 to 7; in each aligned block of 2048 rows (0 to 2047, 2048 to 4095, ...) at most 512 rows name the same one
- slot_cent: int32 [16384], P(('cx', 'cy')), may hold values from 0 to 511
- upper: float32 [4096, 1024], P(('cx', 'cy'), 'rows'), may hold values from -6 to 6
- upper_counts: float32 [4096], P(('cx', 'cy')), may hold values from 1 to 100
Outputs:
- moved: float32 [16384, 1024], P(('cx', 'cy'), 'rows')
- new_counts: float32 [16384], P(('cx', 'cy'))
- new_upper: float32 [4096, 1024], P(('cx', 'cy'), 'rows')
- new_upper_counts: float32 [4096], P(('cx', 'cy'))
Inputs may be any that keep to these rules, and one draw needn't show every extreme that they name: `owner_rows`: the rows of one device name each value at most 16 times, and some device reaches it. `owner_cent`: the 2048 level-1 centroids of one shard name each value at most 512 times, and some shard reaches it.
All inputs are finite; a program needn't handle non-finite values.
Results may differ from a plain program's by a relative error of at most 0.00002.
Values sent between devices are 32-bit elements; how exact they have to be, the bound alone decides.
A program may use at most 64 MiB of HBM per device.

v0:
```python
import functools

import jax
import jax.numpy as jnp
from jax import lax
from jax.experimental import pallas as pl
from jax.experimental.pallas import tpu as pltpu
from jax.sharding import PartitionSpec as P

MESH = pl.DeviceIdType.MESH
LANES = 128
CORES = 2


def exchange_kernel(
    capacity, empty, rows_ref, owner_ref, slot_ref, data, labels,
    info, mine, slabs, packed, inbox, tags, heard,
    si, ri, ss, rs, sp, rp, st, rt,
):
    groups, batch, width = slabs.shape
    shards = inbox.shape[0]
    spots = shards * capacity
    z = lax.axis_index("rows")
    cys = lax.axis_size("cy")
    me = lax.axis_index("cx") * cys + lax.axis_index("cy")

    info[...] = jnp.full_like(info, -1)
    info[0:1, :batch] = owner_ref[...]
    info[1:2, :batch] = slot_ref[...]
    tags[...] = jnp.full_like(tags, empty)

    barrier = pltpu.get_barrier_semaphore()
    mates = [{"rows": lax.rem(z + d, groups)} for d in range(1, groups)]
    peers = []
    for d in range(1, shards):
        t = lax.rem(me + d, shards)
        peers.append({"cx": lax.div(t, cys), "cy": lax.rem(t, cys)})
    for peer in mates + peers:
        pl.semaphore_signal(barrier, inc=1, device_id=peer, device_id_type=MESH)
    pl.semaphore_wait(barrier, groups - 1 + shards - 1)

    def remote(src, dst, send, recv, peer):
        copy = pltpu.make_async_remote_copy(
            src_ref=src, dst_ref=dst, send_sem=send, recv_sem=recv, device_id=peer, device_id_type=MESH
        )
        copy.start()
        return copy

    def columns(group):
        return pl.ds(pl.multiple_of(group * width, width), width)

    asked = [remote(info, mine.at[d], si.at[d - 1], ri.at[d - 1], mates[d - 1]) for d in range(1, groups)]
    sent = [
        remote(
            rows_ref.at[:, columns(mates[d - 1]["rows"])], slabs.at[d],
            ss.at[d - 1], rs.at[d - 1], mates[d - 1],
        )
        for d in range(1, groups)
    ]
    mine[0] = info[...]
    slabs[0] = rows_ref[:, columns(z)]

    bf16, f32 = jnp.bfloat16, jnp.float32
    up = lax.broadcasted_iota(jnp.int32, (LANES, LANES), 0)
    across = lax.broadcasted_iota(jnp.int32, (LANES, LANES), 1)
    before = jnp.where(up < across, 1.0, 0.0).astype(bf16)
    shard_of = lax.broadcasted_iota(jnp.int32, (shards, LANES), 0)
    spot_of = lax.broadcasted_iota(jnp.int32, (spots, LANES), 0)
    line = lax.broadcasted_iota(jnp.int32, (8, LANES), 0)
    moves = []
    for d in range(groups):
        if d:
            asked[d - 1].wait_recv()
        owner, slot = mine[d, 0:1, :], mine[d, 1:2, :]
        named = jnp.where(jnp.broadcast_to(owner, (shards, LANES)) == shard_of, 1.0, 0.0)
        earlier = jnp.dot(named.astype(bf16), before, preferred_element_type=f32)
        position = jnp.sum(named * earlier, axis=0, keepdims=True).astype(jnp.int32)
        target = jnp.where(owner >= 0, owner * capacity + position, -1)
        pick = jnp.where(jnp.broadcast_to(target, (spots, LANES)) == spot_of, 1.0, 0.0).astype(bf16)
        high = jnp.broadcast_to(lax.shift_right_arithmetic(slot, 7), (8, LANES))
        low = jnp.broadcast_to(slot & 127, (8, LANES))
        code = jnp.where(line == 0, high, jnp.where(line == 1, low, 1)).astype(f32).astype(bf16)
        found = lax.dot_general(code, pick, (((1,), (1,)), ((), ())), preferred_element_type=f32)
        tag = (found[0:1] * 128.0 + found[1:2]).astype(jnp.int32)
        tags[d : d + 1, :] = jnp.where(found[2:3] > 0.5, tag, empty)
        if d:
            sent[d - 1].wait_recv()
        slab = slabs[d]
        first = slab.astype(bf16)
        left = slab - first.astype(f32)
        second = left.astype(bf16)
        third = (left - second.astype(f32)).astype(bf16)
        chosen = pick[:, :batch]
        total = jnp.dot(chosen, third, preferred_element_type=f32)
        total = total + jnp.dot(chosen, second, preferred_element_type=f32)
        packed[d] = total + jnp.dot(chosen, first, preferred_element_type=f32)
        for p in range(1, shards):
            t = lax.rem(me + p, shards)
            k = (p - 1) * groups + d
            moves.append(
                remote(
                    packed.at[d, pl.ds(pl.multiple_of(t * capacity, 8), capacity)], inbox.at[p, d],
                    sp.at[k], rp.at[k], peers[p - 1],
                )
            )
    told = [remote(tags, heard.at[p], st.at[p - 1], rt.at[p - 1], peers[p - 1]) for p in range(1, shards)]
    heard[0] = tags[...]
    for d in range(groups):
        inbox[0, d] = packed[d, pl.ds(pl.multiple_of(me * capacity, 8), capacity), :]

    per = LANES // capacity
    lane = lax.broadcasted_iota(jnp.int32, (8, LANES), 1)
    for copy in told:
        copy.wait_recv()
    for g in range(shards // per):
        both = jnp.full((8, LANES), empty, jnp.int32)
        for j in range(per):
            p = g * per + j
            turn = lax.rem((j + shards - me) * capacity, spots)
            turned = pltpu.roll(heard[p], turn, 1)[:, :LANES]
            both = jnp.where((lane >= j * capacity) & (lane < (j + 1) * capacity), turned, both)
        labels[g * groups : (g + 1) * groups, :] = both[:groups]
    for copy in moves:
        copy.wait_recv()
    for p in range(shards):
        g, j = p // per, p % per
        for d in range(groups):
            data[pl.ds((g * groups + d) * LANES + j * capacity, capacity), :] = inbox[p, d]
    for copy in asked + sent + moves + told:
        copy.wait_send()


def exchange(rows_data, owners, slot_rows, lower_rows, width):
    shards = lax.axis_size(("cx", "cy"))
    groups = lax.axis_size("rows")
    batch = rows_data.shape[0]
    capacity = -(-(2 * batch // shards) // 8) * 8
    spots = shards * capacity
    tall = -(-groups // 8) * 8
    vm = pl.BlockSpec(memory_space=pltpu.VMEM)
    f32, i32 = jnp.float32, jnp.int32
    dma = lambda n: pltpu.SemaphoreType.DMA((n,))
    many = (shards - 1) * groups
    return pl.pallas_call(
        functools.partial(exchange_kernel, capacity, lower_rows),
        out_shape=(
            jax.ShapeDtypeStruct((groups * spots, width), f32),
            jax.ShapeDtypeStruct((groups * spots // LANES, LANES), i32),
        ),
        in_specs=[vm] * 3,
        out_specs=(vm, vm),
        scratch_shapes=[
            pltpu.VMEM((8, LANES), i32),
            pltpu.VMEM((groups, 8, LANES), i32),
            pltpu.VMEM((groups, batch, width), f32),
            pltpu.VMEM((groups, spots, width), f32),
            pltpu.VMEM((shards, groups, capacity, width), f32),
            pltpu.VMEM((tall, spots), i32),
            pltpu.VMEM((shards, tall, spots), i32),
            dma(groups - 1), dma(groups - 1), dma(groups - 1), dma(groups - 1),
            dma(many), dma(many), dma(shards - 1), dma(shards - 1),
        ],
        compiler_params=pltpu.CompilerParams(
            collective_id=2, has_side_effects=True, vmem_limit_bytes=16 * 1024 * 1024
        ),
        name="exchange",
    )(rows_data, owners.reshape(1, batch), slot_rows.reshape(1, batch))


def count_columns(ids_row, rows, base, limit):
    spots = lax.broadcasted_iota(jnp.int32, (limit, LANES), 0) + base

    def step(i, total):
        line = jnp.broadcast_to(ids_row(i), (limit, LANES))
        return total + jnp.where(line == spots, 1.0, 0.0)

    total = lax.fori_loop(0, rows, step, jnp.zeros((limit, LANES), jnp.float32))
    return jnp.sum(total, axis=1, keepdims=True)


def eye(size):
    return lax.broadcasted_iota(jnp.int32, (size, size), 0) == lax.broadcasted_iota(jnp.int32, (size, size), 1)


def to_column(row, same):
    size = row.shape[1]
    return jnp.sum(jnp.where(same, jnp.broadcast_to(row, (size, size)), 0.0), axis=1, keepdims=True)


def to_row(column, same):
    size = column.shape[0]
    return jnp.sum(jnp.where(same, jnp.broadcast_to(column, (size, size)), 0.0), axis=0, keepdims=True)


def scatter_rows(tables, source, count, ids):
    many = len(tables)
    steps = LANES // many

    def step(i, _):
        line, first = lax.div(i, steps), lax.rem(i, steps) * many
        for j, table in enumerate(tables):
            table[pl.ds(ids[line, first + j], 1), :] += source[pl.ds(i * many + j, 1), :]
        return 0

    lax.fori_loop(0, count // many, step, 0, unroll=8)


def local_kernel(
    lower_s, upper_s, lower_v, data, cent, counts, moved, news, partial, now, sum0, sum1, t1, t2, t3, sems
):
    for table in (sum0, sum1, partial, t1, t2, t3):
        table[...] = jnp.zeros_like(table)
    scatter_rows((sum0, sum1), data, data.shape[0], lower_s)
    same = eye(LANES)

    def move(b, _):
        here = pl.ds(pl.multiple_of(b * LANES, LANES), LANES)
        m = count_columns(lambda i: lower_v[pl.ds(i, 1), :], lower_v.shape[0], b * LANES, LANES)
        n = to_column(counts[pl.ds(b, 1), :], same) + m
        old = cent[here, :]
        now[here, :] = old + (sum0[here, :] + sum1[here, :] - m * old) / n
        news[pl.ds(b, 1), :] = to_row(n, same)
        return 0

    lax.fori_loop(0, cent.shape[0] // LANES, move, 0)
    put = pltpu.make_async_copy(now, moved, sems.at[0])
    put.start()
    scatter_rows((partial, t1, t2, t3), now, now.shape[0], upper_s)

    def join(b, _):
        here = pl.ds(pl.multiple_of(b * LANES, LANES), LANES)
        partial[here, :] = (partial[here, :] + t1[here, :]) + (t2[here, :] + t3[here, :])
        return 0

    lax.fori_loop(0, partial.shape[0] // LANES, join, 0)
    put.wait()


def local_update(labels, ids, data, centroids, counts, slots):
    rows, width = centroids.shape
    vm = pl.BlockSpec(memory_space=pltpu.VMEM)
    sm = pl.BlockSpec(memory_space=pltpu.SMEM)
    hbm = pl.BlockSpec(memory_space=pl.ANY)
    f32 = jnp.float32
    moved, news, partial = pl.pallas_call(
        local_kernel,
        out_shape=(
            jax.ShapeDtypeStruct((rows, width), f32),
            jax.ShapeDtypeStruct((rows // LANES, LANES), f32),
            jax.ShapeDtypeStruct((slots, width), f32),
        ),
        in_specs=[sm, sm, vm, vm, vm, vm],
        out_specs=(hbm, vm, vm),
        scratch_shapes=[
            pltpu.VMEM((rows, width), f32),
            pltpu.VMEM((rows + 8, width), f32),
            pltpu.VMEM((rows + 8, width), f32),
            pltpu.VMEM((slots, width), f32),
            pltpu.VMEM((slots, width), f32),
            pltpu.VMEM((slots, width), f32),
            pltpu.SemaphoreType.DMA((1,)),
        ],
        compiler_params=pltpu.CompilerParams(vmem_limit_bytes=32 * 1024 * 1024),
        name="local_update",
    )(labels, ids, labels, data, centroids, counts.reshape(-1, LANES))
    return moved, news.reshape(-1), partial


def reduce_kernel(
    ys, xs, part, ids, out, members,
    pair, chip, a1, b1, a2, b2, seen,
    s0, r0, sa1, ra1, sb1, rb1, sa2, ra2, sb2, rb2, si, ri,
):
    y = lax.axis_index("cx")
    cy = lax.axis_index("cy")
    x, core = lax.div(cy, CORES), lax.rem(cy, CORES)
    cys = xs * CORES
    shards = ys * cys
    me = y * cys + cy
    slots = part.shape[1]
    half = slots // 2
    lines = ids.shape[0]

    barrier = pltpu.get_barrier_semaphore()
    peers = []
    for d in range(1, shards):
        t = lax.rem(me + d, shards)
        peers.append({"cx": lax.div(t, cys), "cy": lax.rem(t, cys)})
    for peer in peers:
        pl.semaphore_signal(barrier, inc=1, device_id=peer, device_id_type=MESH)
    pl.semaphore_wait(barrier, shards - 1)

    def remote(src, dst, send, recv, peer):
        copy = pltpu.make_async_remote_copy(
            src_ref=src, dst_ref=dst, send_sem=send, recv_sem=recv, device_id=peer, device_id_type=MESH
        )
        copy.start()
        return copy

    offsets = [(dy, dx) for dy in range(ys) for dx in range(xs)]
    offsets.sort(key=lambda o: -((o[0] != 0) * 2 + (o[1] != 0) * 2))

    def at(dy, dx):
        return lax.rem(y + dy, ys), lax.rem(x + dx, xs)

    started = []
    first = {}
    for dy, dx in offsets:
        ty, tx = at(dy, dx)
        k = dy * xs + dx
        first[dy, dx] = remote(
            part.at[(ty * xs + tx) * CORES + 1 - core], pair.at[k], s0.at[k], r0.at[k],
            {"cx": y, "cy": x * CORES + 1 - core},
        )
    idc = [remote(ids, seen.at[d], si.at[d - 1], ri.at[d - 1], peers[d - 1]) for d in range(1, shards)]
    seen[0] = ids[...]

    ac, bc = {}, {}
    for dy, dx in offsets:
        ty, tx = at(dy, dx)
        k = dy * xs + dx
        first[dy, dx].wait_recv()
        chip[k] = part[(ty * xs + tx) * CORES + core] + pair[k]
        if dy:
            ac[dy, dx] = remote(
                chip.at[k, pl.ds(0, half)], a1.at[(dy - 1) * xs + dx],
                sa1.at[(dy - 1) * xs + dx], ra1.at[(dy - 1) * xs + dx],
                {"cx": ty, "cy": cy},
            )
        if dx:
            bc[dy, dx] = remote(
                chip.at[k, pl.ds(half, half)], b1.at[(dx - 1) * ys + dy],
                sb1.at[(dx - 1) * ys + dy], rb1.at[(dx - 1) * ys + dy],
                {"cx": y, "cy": tx * CORES + core},
            )

    a2c, b2c = {}, {}
    for dx in range(1, xs):
        for dy in range(1, ys):
            ac[dy, dx].wait_recv()
        total = chip[dx, :half]
        for dy in range(1, ys):
            total = total + a1[(dy - 1) * xs + dx]
        chip[dx, :half] = total
        a2c[dx] = remote(
            chip.at[dx, pl.ds(0, half)], a2.at[dx - 1], sa2.at[dx - 1], ra2.at[dx - 1],
            {"cx": y, "cy": lax.rem(x + dx, xs) * CORES + core},
        )
    for dy in range(1, ys):
        for dx in range(1, xs):
            bc[dy, dx].wait_recv()
        total = chip[dy * xs, half:]
        for dx in range(1, xs):
            total = total + b1[(dx - 1) * ys + dy]
        chip[dy * xs, half:] = total
        b2c[dy] = remote(
            chip.at[dy * xs, pl.ds(half, half)], b2.at[dy - 1], sb2.at[dy - 1], rb2.at[dy - 1],
            {"cx": lax.rem(y + dy, ys), "cy": cy},
        )

    for copy in idc:
        copy.wait_recv()
    block = min(LANES, slots)
    for b in range(slots // block):
        here = pl.ds(b * block, block)
        m = count_columns(
            lambda i: seen[lax.div(i, lines), pl.ds(lax.rem(i, lines), 1), :],
            shards * lines, me * slots + b * block, block,
        )
        members[here, :] = jnp.broadcast_to(m, (block, LANES))

    for dy in range(1, ys):
        ac[dy, 0].wait_recv()
    for dx in range(1, xs):
        bc[0, dx].wait_recv()
    for dx in range(1, xs):
        a2c[dx].wait_recv()
    for dy in range(1, ys):
        b2c[dy].wait_recv()

    total = chip[0, :half]
    for dy in range(1, ys):
        total = total + a1[(dy - 1) * xs]
    for dx in range(1, xs):
        total = total + a2[dx - 1]
    out[:half, :] = total
    total = chip[0, half:]
    for dx in range(1, xs):
        total = total + b1[(dx - 1) * ys]
    for dy in range(1, ys):
        total = total + b2[dy - 1]
    out[half:, :] = total

    for group in (first.values(), idc, ac.values(), bc.values(), a2c.values(), b2c.values()):
        for copy in group:
            copy.wait_send()


def finish_kernel(total, members, upper, weights, out, news):
    lines, block = weights.shape
    same = eye(block)
    for b in range(lines):
        here = pl.ds(b * block, block)
        m = members[here, :1]
        n = to_column(weights[b : b + 1, :], same) + m
        prev = upper[here, :]
        out[here, :] = prev + (total[here, :] - m * prev) / n
        news[b : b + 1, :] = to_row(n, same)


def reduce_update(partial, ids, upper, weights, ys, xs):
    slots, width = upper.shape
    half = slots // 2
    block = min(LANES, slots)
    shards = ys * xs * CORES
    vm = pl.BlockSpec(memory_space=pltpu.VMEM)
    f32 = jnp.float32
    n0, na, nb = ys * xs, (ys - 1) * xs, (xs - 1) * ys
    dma = lambda n: pltpu.SemaphoreType.DMA((n,))
    total, members = pl.pallas_call(
        functools.partial(reduce_kernel, ys, xs),
        out_shape=(
            jax.ShapeDtypeStruct((slots, width), f32),
            jax.ShapeDtypeStruct((slots, LANES), f32),
        ),
        in_specs=[vm] * 2,
        out_specs=(vm, vm),
        scratch_shapes=[
            pltpu.VMEM((n0, slots, width), f32),
            pltpu.VMEM((n0, slots, width), f32),
            pltpu.VMEM((na, half, width), f32),
            pltpu.VMEM((nb, half, width), f32),
            pltpu.VMEM((xs - 1, half, width), f32),
            pltpu.VMEM((ys - 1, half, width), f32),
            pltpu.VMEM((shards,) + ids.shape, jnp.int32),
            dma(n0), dma(n0), dma(na), dma(na), dma(nb), dma(nb),
            dma(xs - 1), dma(xs - 1), dma(ys - 1), dma(ys - 1),
            dma(shards - 1), dma(shards - 1),
        ],
        compiler_params=pltpu.CompilerParams(
            collective_id=1, has_side_effects=True, vmem_limit_bytes=20 * 1024 * 1024
        ),
        name="reduce_update",
    )(
        partial.reshape(shards, slots, width),
        ids,
    )
    new_upper, news = pl.pallas_call(
        finish_kernel,
        out_shape=(
            jax.ShapeDtypeStruct((slots, width), f32),
            jax.ShapeDtypeStruct((slots // block, block), f32),
        ),
        in_specs=[vm] * 4,
        out_specs=(vm, vm),
        compiler_params=pltpu.CompilerParams(vmem_limit_bytes=8 * 1024 * 1024),
        name="finish",
    )(total, members, upper, weights.reshape(-1, block))
    return new_upper, news.reshape(-1)


def body(
    rows_data, owner_rows, slot_rows, centroids, counts, owner_cent, slot_cent, upper, upper_counts
):
    ys, xs = lax.axis_size("cx"), lax.axis_size("cy") // CORES
    upper_rows = upper.shape[0]
    ids = (owner_cent[:, 0] * upper_rows + slot_cent).reshape(-1, LANES)
    data, labels = exchange(rows_data, owner_rows, slot_rows, *centroids.shape)
    moved, new_counts, partial = local_update(
        labels, ids, data, centroids, counts, upper_rows * ys * xs * CORES
    )
    new_upper, new_upper_counts = reduce_update(partial, ids, upper, upper_counts, ys, xs)
    return (moved, new_counts, new_upper, new_upper_counts)


def solution(mesh):
    placed = (
        P(("rows", "cx", "cy"), None),
        P(("rows", "cx", "cy"), None),
        P(("rows", "cx", "cy")),
        P(("cx", "cy"), "rows"),
        P(("cx", "cy")),
        P(("cx", "cy"), None),
        P(("cx", "cy")),
        P(("cx", "cy"), "rows"),
        P(("cx", "cy")),
    )
    return jax.shard_map(
        body,
        mesh=mesh,
        in_specs=placed,
        out_specs=(
            P(("cx", "cy"), "rows"),
            P(("cx", "cy")),
            P(("cx", "cy"), "rows"),
            P(("cx", "cy")),
        ),
        check_vma=False,
    )
```

profile of v0, /device:TPU:0, one launch (start us, length us, event | category | flops | bytes accessed | tf_op | source)
XLA Modules:
  0.0 69.3 jit_solution(4421432982625457996)
XLA Ops:
  0.6 0.7 %broadcast_multiply_fusion = s32[2048,1]{0,1:T(1,128)S(1)} fusion(s32[2048,1]{0,1:T(1,128)} %param.14), kind=kLoop, calls=%fused_computation.1 | loop fusion | flops 2048 | bytes 16384 | tf_op jit(solution)/shard_map/mul | solution.py:467
  1.3 0.7 %add_bitcast_fusion.upper_s.ids = s32[16,128]{1,0:T(8,128)S(1)} fusion(s32[2048]{0:T(1024)S(1)} %bitcast.15, s32[2048]{0:T(1024)} %param.15), kind=kLoop, calls=%fused_computation | loop fusion | flops 2048 | bytes 24576 | tf_op jit(solution)/shard_map/reshape | solution.py:467
  2.0 0.0 copy-start.2
  2.0 0.9 %copy-done.2 = f32[64,1024]{1,0:T(8,128)S(1)} copy-done((f32[64,1024]{1,0:T(8,128)S(1)}, f32[64,1024]{1,0:T(8,128)}, u32[]{:S(2)}) %copy-start.2) | copy-done | bytes 262168
  3.0 0.0 copy-start.5
  3.0 0.7 copy-done.5
  3.6 0.0 copy-start.6
  3.6 0.7 copy-done.6
  4.3 17.9 %exchange.1 = (f32[512,256]{1,0:T(8,128)S(1)}, s32[4,128]{1,0:T(4,128)S(1)}) custom-call(f32[64,1024]{1,0:T(8,128)S(1)} %copy-done.2, s32[1,64]{1,0:T(1,128)S(1)} %bitcast.13, s32[1,64]{1,0:T(1,128)S(1)} %bitcast.14), custom_call_target="tpu_custom_call" | custom-call | tf_op jit(solution)/shard_map/exchange/pallas_call | solution.py:144
  22.2 0.0 copy-start
  22.2 1.6 %copy-done = f32[2048,256]{1,0:T(8,128)S(1)} copy-done((f32[2048,256]{1,0:T(8,128)S(1)}, f32[2048,256]{1,0:T(8,128)}, u32[]{:S(2)}) %copy-start) | copy-done | bytes 2097176
  23.8 0.0 copy-start.3
  23.8 0.7 %copy-done.3 = f32[2048]{0:T(1024)S(1)} copy-done((f32[2048]{0:T(1024)S(1)}, f32[2048]{0:T(1024)}, u32[]{:S(2)}) %copy-start.3) | copy-done | bytes 8216
  24.5 20.9 %local_update.1 = (f32[2048,256]{1,0:T(8,128)}, f32[16,128]{1,0:T(8,128)}, f32[4096,256]{1,0:T(8,128)S(1)}) custom-call(s32[4,128]{1,0:T(4,128)S(1)} %get-tuple-element.13.lower_s.lower_v, s32[16,128]{1,0:T(8,128)S(1)} %add_bitcast_fusion.upper_s.ids, s32[4,128]{1,0:T(4,128)S(1)} %get-tuple-element.13.lower_s.lower_v, ...), custom_call_target="tpu_custom_call" | custom-call | tf_op jit(solution)/shard_map/local_update/pallas_call | solution.py:245
  45.4 0.0 copy-start.1
  45.4 0.0 copy-start.4
  45.4 22.7 %reduce_update.1 = (f32[512,256]{1,0:T(8,128)S(1)}, f32[512,128]{1,0:T(8,128)S(1)}) custom-call(f32[8,512,256]{2,1,0:T(8,128)S(1)} %bitcast.10, s32[16,128]{1,0:T(8,128)S(1)} %add_bitcast_fusion.upper_s.ids), custom_call_target="tpu_custom_call" | custom-call | tf_op jit(solution)/shard_map/reduce_update/pallas_call | solution.py:420
  68.2 0.0 copy-done.1
  68.2 0.0 copy-done.4
  68.2 1.1 %finish.1 = (f32[512,256]{1,0:T(8,128)}, f32[4,128]{1,0:T(4,128)}) custom-call(f32[512,256]{1,0:T(8,128)S(1)} %get-tuple-element.18.total, f32[512,128]{1,0:T(8,128)S(1)} %get-tuple-element.19.members, f32[512,256]{1,0:T(8,128)S(1)} %copy-done.1, f32[4,128]{1,0:T(4,128)S(1)} %bitcast.12), custom_call_target="tpu_custom_call" | custom-call | tf_op jit(solution)/shard_map/finish/pallas_call | solution.py:448
Async XLA Ops:
  2.0 0.9 %copy-start.2 = (f32[64,1024]{1,0:T(8,128)S(1)}, f32[64,1024]{1,0:T(8,128)}, u32[]{:S(2)}) copy-start(f32[64,1024]{1,0:T(8,128)} %rows_ref.1) | copy-start | bytes 786436
  3.0 0.7 copy-start.5
  3.6 0.7 copy-start.6
  22.2 1.6 %copy-start = (f32[2048,256]{1,0:T(8,128)S(1)}, f32[2048,256]{1,0:T(8,128)}, u32[]{:S(2)}) copy-start(f32[2048,256]{1,0:T(8,128)} %cent.1) | copy-start | bytes 6291460
  23.8 0.7 %copy-start.3 = (f32[2048]{0:T(1024)S(1)}, f32[2048]{0:T(1024)}, u32[]{:S(2)}) copy-start(f32[2048]{0:T(1024)} %param.13) | copy-start | bytes 24580
  45.4 22.7 %copy-start.1 = (f32[512,256]{1,0:T(8,128)S(1)}, f32[512,256]{1,0:T(8,128)}, u32[]{:S(2)}) copy-start(f32[512,256]{1,0:T(8,128)} %upper.1) | copy-start | bytes 1572868
  45.4 22.7 %copy-start.4 = (f32[512]{0:T(512)S(1)}, f32[512]{0:T(512)}, u32[]{:S(2)}) copy-start(f32[512]{0:T(512)} %param.17) | copy-start | bytes 6148
where the time goes:
time: 69.6 us; the launch traced here: 69.3 us
  Pallas kernels  62.6 us (90%)
  local copies, waits for them, and re-layouts  4.55 us (7%)
  other arithmetic  1.4 us (2%)
  between operations  0.7 us (1%)
    pallas_call x1, Pallas kernels, reduce_update(): pl.pallas_call(functools.partial(reduce_kernel, ys, xs), out_shape=(jax.S...  22.7 us
    pallas_call x1, Pallas kernels, local_update(): pl.pallas_call(local_kernel, out_shape=(jax.ShapeDtypeStruct((rows, width...  20.9 us
    pallas_call x1, Pallas kernels, exchange(): pl.pallas_call(functools.partial(exchange_kernel, capacity, lower_rows),...  17.9 us
    unnamed x14, local copies, waits for them, and re-layouts  4.55 us

commit v1 on v0

v1 whole, which is shorter than its diff:
```python
import functools
import types

import jax
import jax.numpy as jnp
from jax import lax
from jax.experimental import pallas as pl
from jax.experimental.pallas import tpu as pltpu
from jax.sharding import PartitionSpec as P

MESH = pl.DeviceIdType.MESH
LANES = 128
CORES = 2
SPAN = 256
bf16, f32, i32 = jnp.bfloat16, jnp.float32, jnp.int32


def pieces(x):
    first = x.astype(bf16)
    return first, (x - first.astype(f32)).astype(bf16)


def halves(x):
    return x[:, :LANES] + x[:, LANES : 2 * LANES]


def square(size):
    up = lax.broadcasted_iota(i32, (size, size), 0)
    return up == lax.broadcasted_iota(i32, (size, size), 1)


def to_column(row, same):
    size = row.shape[1]
    return jnp.sum(jnp.where(same, jnp.broadcast_to(row, (size, size)), 0.0), axis=1, keepdims=True)


def to_row(column, same):
    return jnp.sum(jnp.where(same, jnp.broadcast_to(column, same.shape), 0.0), axis=0, keepdims=True)


def each(count, step):
    if count == 1:
        step(0)
    elif count > 1:
        lax.fori_loop(0, count, lambda e, c: (step(e), c)[1], 0)


def one_hot(row_of, lines, out, height):
    span = min(SPAN, height)
    spots = lax.broadcasted_iota(i32, (span, LANES), 0).astype(f32).astype(bf16)
    one, zero = jnp.ones((span, LANES), bf16), jnp.zeros((span, LANES), bf16)
    for q in range(height // span):
        for b in range(lines):
            row = jnp.broadcast_to(row_of(b) - float(q * span), (16, LANES)).astype(bf16)
            row = jnp.concatenate([row] * (span // 16), axis=0)
            out[q * span : (q + 1) * span, b * LANES : (b + 1) * LANES] = jnp.where(row == spots, one, zero)


def fused_kernel(
    names, sizes, rows_h, owner_h, slot_h, cent_h, counts_h, oc_h, sc_h, upper_h, weights_h,
    moved, news, newup, upnews, *scratch,
):
    s = types.SimpleNamespace(**dict(zip(names, scratch)))
    zs, ys, xs, capacity, height = sizes
    chips, cys = ys * xs, xs * CORES
    shards = chips * CORES
    batch = rows_h.shape[0]
    count, width = cent_h.shape
    parts = width // LANES
    lines = count // LANES
    slots = upper_h.shape[0]
    half = slots // 2
    tall, block = weights_h.shape
    spots = shards * capacity
    per = LANES // capacity
    across = zs * spots // LANES
    joined = across * LANES

    z, y, cy = lax.axis_index("rows"), lax.axis_index("cx"), lax.axis_index("cy")
    x, core = lax.div(cy, CORES), lax.rem(cy, CORES)
    me = y * cys + cy
    other = {"cx": y, "cy": x * CORES + 1 - core}

    def mate(d):
        if zs & (zs - 1):
            return lax.rem(z + d, zs)
        at = z
        bit = 1
        while bit <= d:
            if d & bit:
                at = at + bit * (1 - 2 * lax.rem(lax.div(z, bit), 2))
            bit *= 2
        return at

    mates = {d: {"rows": mate(d)} for d in range(1, zs)}
    peers = {}
    for p in range(1, shards):
        t = lax.rem(me + p, shards)
        peers[p] = {"cx": lax.div(t, cys), "cy": lax.rem(t, cys)}

    barrier = pltpu.get_barrier_semaphore()
    for peer in list(mates.values()) + list(peers.values()):
        pl.semaphore_signal(barrier, inc=1, device_id=peer, device_id_type=MESH)

    loads = [
        pltpu.make_async_copy(src, dst, s.ld.at[i])
        for i, (src, dst) in enumerate([
            (oc_h, s.oc), (sc_h, s.sc), (cent_h, s.cent), (owner_h, s.owner), (slot_h, s.slot),
            (rows_h, s.rows), (counts_h, s.counts), (upper_h, s.upper), (weights_h, s.weights),
        ])
    ]
    for copy in loads:
        copy.start()

    def remote(src, dst, send, recv, peer):
        return pltpu.make_async_remote_copy(
            src_ref=src, dst_ref=dst, send_sem=send, recv_sem=recv, device_id=peer, device_id_type=MESH
        )

    def started(*args):
        copy = remote(*args)
        copy.start()
        return copy

    same = square(LANES)
    lane = lax.broadcasted_iota(i32, (LANES, LANES), 1)

    regions = {
        "diag": ((ys - 1) * (xs - 1), lambda e: (1 + lax.div(e, xs - 1), 1 + lax.rem(e, xs - 1))),
        "dy": (ys - 1, lambda e: (1 + e, 0)),
        "dx": (xs - 1, lambda e: (0, 1 + e)),
        "own": (1, lambda e: (0, 0)),
    }

    def region(name, step):
        number, where = regions[name]

        def run(e):
            if isinstance(e, int):
                e = jnp.int32(e)
            step(*where(e))

        each(number, run)

    def shard_at(dy, dx, side):
        return (lax.rem(y + dy, ys) * xs + lax.rem(x + dx, xs)) * CORES + side

    loads[0].wait()
    loads[1].wait()
    for b in range(lines):
        s.own[b : b + 1, :] = s.oc[0:1, b * LANES : (b + 1) * LANES]
    s.uid[...] = (s.own[...] * slots + s.sc[...]).astype(f32)
    loads[2].wait()

    def split(b, c):
        here = pl.ds(pl.multiple_of(b * SPAN, SPAN), SPAN)
        for h in range(parts):
            hi, lo = pieces(s.cent[here, h * LANES : (h + 1) * LANES])
            s.cp[h, here, :LANES] = hi
            s.cp[h, here, LANES:] = lo
        return c

    lax.fori_loop(0, count // SPAN, split, 0)

    def pair(k, h):
        i = h * chips + k
        return remote(s.outp.at[i], s.pair.at[i], s.sb.at[i], s.rb.at[i], other)

    def base(h, share=True):
        def step(dy, dx):
            k = dy * xs + dx
            i = h * chips + k
            for mine_too, side in ((0, 1 - core), (1, core)):
                first = (shard_at(dy, dx, side) * slots).astype(f32)
                one_hot(lambda b: s.uid[b : b + 1, :] - first, lines, s.oh.at[mine_too], slots)
                total = halves(jnp.dot(s.oh[mine_too], s.cp[h], preferred_element_type=f32))
                if mine_too:
                    s.base[i] = total
                else:
                    s.outp[i] = total
                    if share:
                        pair(k, h).start()

        return step

    region("diag", base(0, False))

    loads[3].wait()
    loads[4].wait()
    loads[5].wait()
    s.info[...] = jnp.full_like(s.info, -1)
    s.info[0:1, :batch] = s.owner[...]
    s.info[1:2, :batch] = s.slot[...]
    s.tags[...] = jnp.full_like(s.tags, count)
    pl.semaphore_wait(barrier, zs - 1 + shards - 1)
    region("diag", lambda dy, dx: pair(dy * xs + dx, 0).start())

    order = list(range(zs - 1, 0, -1))
    asked, sent = {}, {}
    for d in order:
        asked[d] = started(s.info, s.mine.at[d], s.si.at[d - 1], s.ri.at[d - 1], mates[d])
    for h in range(parts):
        for d in order:
            here = pl.ds(pl.multiple_of(mates[d]["rows"] * width + h * LANES, LANES), LANES)
            i = h * (zs - 1) + d - 1
            sent[h, d] = started(s.rows.at[:, here], s.slabs.at[h * zs + d], s.ss.at[i], s.rs.at[i], mates[d])
    s.mine[0] = s.info[...]
    for h in range(parts):
        s.slabs[h * zs] = s.rows[:, pl.ds(pl.multiple_of(z * width + h * LANES, LANES), LANES)]

    before = jnp.where(lax.broadcasted_iota(i32, (LANES, LANES), 0) < lane, 1.0, 0.0).astype(bf16)
    shard_of = lax.broadcasted_iota(i32, (shards, LANES), 0)
    spot_of = lax.broadcasted_iota(i32, (spots, LANES), 0)
    line_of = lax.broadcasted_iota(i32, (8, LANES), 0)

    def place(d):
        owner, slot = s.mine[d, 0:1, :], s.mine[d, 1:2, :]
        named = jnp.where(jnp.broadcast_to(owner, (shards, LANES)) == shard_of, 1.0, 0.0)
        earlier = jnp.dot(named.astype(bf16), before, preferred_element_type=f32)
        position = jnp.sum(named * earlier, axis=0, keepdims=True).astype(i32)
        target = jnp.where(owner >= 0, owner * capacity + position, -1)
        pick = jnp.where(jnp.broadcast_to(target, (spots, LANES)) == spot_of, 1.0, 0.0).astype(bf16)
        s.pick[d] = pick
        high = jnp.broadcast_to(lax.shift_right_arithmetic(slot, 7), (8, LANES))
        low = jnp.broadcast_to(slot & 127, (8, LANES))
        code = jnp.where(line_of == 0, high, jnp.where(line_of == 1, low, 1)).astype(f32).astype(bf16)
        found = lax.dot_general(code, pick, (((1,), (1,)), ((), ())), preferred_element_type=f32)
        tag = (found[0:1] * 128.0 + found[1:2]).astype(i32)
        s.tags[d : d + 1, :] = jnp.where(found[2:3] > 0.5, tag, count)

    def spot(p, d):
        return ((p // per) * zs + d) * LANES + (p % per) * capacity

    moves = {}

    def pack(d, h):
        slab = s.slabs[h * zs + d]
        hi, mid = pieces(slab)
        low = (slab - hi.astype(f32) - mid.astype(f32)).astype(bf16)
        three = jnp.concatenate([hi, mid, low], axis=1)
        total = jnp.dot(s.pick[d, :, :batch], three, preferred_element_type=f32)
        total = (total[:, 2 * LANES :] + total[:, LANES : 2 * LANES]) + total[:, :LANES]
        s.packed[h * zs + d] = total
        for p in range(1, shards):
            t = lax.rem(me + p, shards)
            i = ((p - 1) * zs + d) * parts + h
            moves[p, d, h] = started(
                s.packed.at[h * zs + d, pl.ds(pl.multiple_of(t * capacity, 8), capacity)],
                s.inbox.at[h, pl.ds(spot(p, d), capacity)], s.sp.at[i], s.rp.at[i], peers[p],
            )
        s.inbox[h, spot(0, d) : spot(0, d) + capacity, :] = s.packed[
            h * zs + d, pl.ds(pl.multiple_of(me * capacity, 8), capacity), :
        ]

    place(0)
    for h in range(parts):
        pack(0, h)

    region("dy", base(0))

    for d in range(1, zs):
        asked[d].wait_recv()
    for d in range(1, zs):
        place(d)
    told = {p: started(s.tags, s.heard.at[p], s.st.at[p - 1], s.rt.at[p - 1], peers[p]) for p in range(1, shards)}
    s.heard[0] = s.tags[...]

    region("dx", base(0))

    for h in range(parts):
        for d in range(1, zs):
            sent[h, d].wait_recv()
            pack(d, h)

    high = s.own[...] * 8 + lax.div(s.sc[...], block)
    low = lax.rem(s.sc[...], block)
    tile_of = lax.broadcasted_iota(i32, (shards * 8, LANES), 0)
    down = lax.broadcasted_iota(i32, (LANES, LANES), 0)
    for b in range(lines):
        here = slice(b * LANES, (b + 1) * LANES)
        s.ha[:, here] = jnp.where(
            jnp.broadcast_to(high[b : b + 1, :], (shards * 8, LANES)) == tile_of, 1.0, 0.0
        ).astype(bf16)
        s.hb[:, here] = jnp.where(
            jnp.broadcast_to(low[b : b + 1, :], (LANES, LANES)) == down, 1.0, 0.0
        ).astype(bf16)
    s.hist[...] = lax.dot_general(s.ha[...], s.hb[...], (((1,), (1,)), ((), ())), preferred_element_type=f32)
    tallied = {}
    for p in range(1, shards):
        t = lax.rem(me + p, shards)
        tallied[p] = started(
            s.hist.at[pl.ds(pl.multiple_of(t * 8, 8), 8)], s.hs.at[p], s.sh.at[p - 1], s.rh.at[p - 1], peers[p]
        )
    s.hs[0] = s.hist[pl.ds(pl.multiple_of(me * 8, 8), 8), :]

    loads[6].wait()
    for p in range(1, shards):
        told[p].wait_recv()
    few = lax.broadcasted_iota(i32, (s.tags.shape[0], LANES), 1)
    s.lab[...] = jnp.full_like(s.lab, count)
    for g in range(shards // per):
        both = jnp.full(few.shape, count, i32)
        for j in range(per):
            turn = lax.rem((j + shards - me) * capacity, spots)
            turned = pltpu.roll(s.heard[g * per + j], turn, 1)[:, :LANES]
            both = jnp.where((few >= j * capacity) & (few < (j + 1) * capacity), turned, both)
        s.lab[g * zs : (g + 1) * zs, :] = both[:zs].astype(f32)

    band = s.ot.shape[0]

    def gather(jb, c):
        for rr in range(band // LANES):
            r = jb * (band // LANES) + rr
            here = pl.ds(pl.multiple_of(r * LANES, LANES), LANES)
            row = s.lab[pl.ds(r, 1), :]
            label = jnp.broadcast_to(to_column(row, same), (LANES, LANES))

            def alike(q, total):
                return total + jnp.where(label == s.lab[pl.ds(q, 1), :], 1.0, 0.0)

            mates_of = lax.fori_loop(0, across, alike, jnp.zeros((LANES, LANES), f32), unroll=min(across, 4))
            had, named = jnp.zeros((LANES, LANES), f32), jnp.zeros((LANES, LANES), f32)
            for b in range(lines):
                hit = label == (lane + b * LANES).astype(f32)
                s.ot[rr * LANES : (rr + 1) * LANES, b * LANES : (b + 1) * LANES] = jnp.where(hit, 1.0, 0.0).astype(bf16)
                had = had + jnp.where(hit, s.counts[b : b + 1, :], 0.0)
                named = named + jnp.where(hit, s.uid[b : b + 1, :], 0.0)
            n = jnp.sum(had + mates_of, axis=1, keepdims=True)
            s.share[here, :] = jnp.broadcast_to(1.0 / n, (LANES, LANES))
            target = to_row(jnp.sum(named, axis=1, keepdims=True), same)
            s.urow[pl.ds(r, 1), :] = jnp.where(row < float(count), target, -1.0)
        for h in range(parts):
            s.near[h, pl.ds(pl.multiple_of(jb * band, band), band), :] = halves(
                jnp.dot(s.ot[...], s.cp[h], preferred_element_type=f32)
            )
        return c

    s.urow[...] = jnp.full_like(s.urow, -1.0)
    each(joined // band, lambda jb: gather(jb, 0))
    linked = started(s.urow, s.prow, s.su.at[0], s.ru.at[0], other)

    def give(h):
        return remote(s.dl.at[h], s.pd.at[h], s.sd.at[h], s.rd.at[h], other)

    def change(h):
        for p in range(1, shards):
            for d in range(zs):
                moves[p, d, h].wait_recv()

        def step(e):
            here = pl.ds(e * SPAN, SPAN)
            s.dl[h, here, :] = (s.inbox[h, here, :] - s.near[h, here, :]) * s.share[here, :]

        each(joined // SPAN, step)
        give(h).start()

        def cut(e):
            here = pl.ds(e * SPAN, SPAN)
            hi, lo = pieces(s.dl[h, here, :])
            s.dd[h, here, :LANES] = hi
            s.dd[h, here, LANES:] = lo

        each(joined // SPAN, cut)

    def accept(h):
        give(h).wait_recv()

        def cut(e):
            here = pl.ds(e * SPAN, SPAN)
            there = pl.ds(e * SPAN + joined, SPAN)
            hi, lo = pieces(s.pd[h, here, :])
            s.dd[h, there, :LANES] = hi
            s.dd[h, there, LANES:] = lo

        each(joined // SPAN, cut)

    def at(dy, dx):
        return lax.rem(y + dy, ys), lax.rem(x + dx, xs)

    na, nb = (ys - 1) * xs, (xs - 1) * ys

    def a1(dy, dx, h):
        i = h * na + (dy - 1) * xs + dx
        return remote(
            s.chip.at[h * chips + dy * xs + dx, pl.ds(0, half)], s.a1.at[i], s.sa1.at[i], s.ra1.at[i],
            {"cx": lax.rem(y + dy, ys), "cy": cy},
        )

    def b1(dy, dx, h):
        i = h * nb + (dx - 1) * ys + dy
        return remote(
            s.chip.at[h * chips + dy * xs + dx, pl.ds(half, half)], s.b1.at[i], s.sb1.at[i], s.rb1.at[i],
            {"cx": y, "cy": lax.rem(x + dx, xs) * CORES + core},
        )

    def a2(dx, h):
        i = h * (xs - 1) + dx - 1
        return remote(
            s.relay_a.at[i], s.a2.at[i], s.sa2.at[i], s.ra2.at[i],
            {"cx": y, "cy": lax.rem(x + dx, xs) * CORES + core},
        )

    def b2(dy, h):
        i = h * (ys - 1) + dy - 1
        return remote(
            s.relay_b.at[i], s.b2.at[i], s.sb2.at[i], s.rb2.at[i],
            {"cx": lax.rem(y + dy, ys), "cy": cy},
        )

    def combine(h, name):
        def step(dy, dx):
            k = dy * xs + dx
            i = h * chips + k
            first = (shard_at(dy, dx, core) * slots).astype(f32)
            one_hot(
                lambda b: (s.urow[b : b + 1, :] if b < across else s.prow[b - across : b - across + 1, :]) - first,
                2 * across, s.oh3, slots,
            )
            pair(k, h).wait_recv()
            total = halves(jnp.dot(s.oh3[...], s.dd[h], preferred_element_type=f32))
            s.chip[i] = total + (s.base[i] + s.pair[i])
            if name in ("diag", "dy"):
                a1(dy, dx, h).start()
            if name in ("diag", "dx"):
                b1(dy, dx, h).start()

        region(name, step)

    def forward(h):
        for dx in range(1, xs):
            i = h * chips + dx
            total = s.chip[i, :half]
            for dy in range(1, ys):
                a1(dy, dx, h).wait_recv()
                total = total + s.a1[h * na + (dy - 1) * xs + dx]
            s.relay_a[h * (xs - 1) + dx - 1] = total
            a2(dx, h).start()
        for dy in range(1, ys):
            i = h * chips + dy * xs
            total = s.chip[i, half:]
            for dx in range(1, xs):
                b1(dy, dx, h).wait_recv()
                total = total + s.b1[h * nb + (dx - 1) * ys + dy]
            s.relay_b[h * (ys - 1) + dy - 1] = total
            b2(dy, h).start()

    change(0)
    for h in range(1, parts):
        region("diag", base(h))
    linked.wait_recv()
    accept(0)
    for name in ("diag", "dy", "dx"):
        combine(0, name)
    for h in range(1, parts):
        region("dy", base(h))
        region("dx", base(h))
        change(h)
        if h == 1:
            region("own", base(0))
        accept(h)
        for name in ("diag", "dy", "dx"):
            combine(h, name)
    if parts == 1:
        region("own", base(0))
    combine(0, "own")
    forward(0)

    loads[7].wait()
    loads[8].wait()

    def lay(e):
        here = pl.ds(e * SPAN, SPAN)
        for h in range(parts):
            hi, lo = pieces(s.inbox[h, here, :])
            s.dp[here, 2 * h * LANES : (2 * h + 1) * LANES] = hi
            s.dp[here, (2 * h + 1) * LANES : (2 * h + 2) * LANES] = lo
        s.dp[here, 2 * parts * LANES :] = jnp.ones((SPAN, LANES), bf16)

    each(joined // SPAN, lay)

    def move(e):
        first = (jnp.int32(e) * height).astype(f32)
        one_hot(lambda b: s.lab[b : b + 1, :] - first, across, s.oh1, height)
        s.sums[...] = jnp.dot(s.oh1[...], s.dp[...], preferred_element_type=f32)
        for sub in range(height // LANES):
            b = e * (height // LANES) + sub
            here = pl.ds(pl.multiple_of(b * LANES, LANES), LANES)
            local = slice(sub * LANES, (sub + 1) * LANES)
            m = s.sums[local, 2 * parts * LANES :]
            n = to_column(s.counts[pl.ds(b, 1), :], same) + m
            r = 1.0 / n
            for h in range(parts):
                total = s.sums[local, 2 * h * LANES : (2 * h + 1) * LANES] + s.sums[
                    local, (2 * h + 1) * LANES : (2 * h + 2) * LANES
                ]
                old = s.cent[here, h * LANES : (h + 1) * LANES]
                moved[here, h * LANES : (h + 1) * LANES] = old + (total - m * old) * r
            news[pl.ds(b, 1), :] = to_row(n, same)

    each(count // height, move)

    for h in range(1, parts):
        region("own", base(h))
        combine(h, "own")
        forward(h)

    tally = s.hs[0]
    for p in range(1, shards):
        tallied[p].wait_recv()
        tally = tally + s.hs[p]
    members = tally[:tall, :block]
    upnews[...] = s.weights[...] + members
    square_block = square(block)

    def finish(h):
        base_i = h * chips
        for dy in range(1, ys):
            a1(dy, 0, h).wait_recv()
        for dx in range(1, xs):
            b1(0, dx, h).wait_recv()
        for dx in range(1, xs):
            a2(dx, h).wait_recv()
        for dy in range(1, ys):
            b2(dy, h).wait_recv()
        total = s.chip[base_i, :half]
        for dy in range(1, ys):
            total = total + s.a1[h * na + (dy - 1) * xs]
        for dx in range(1, xs):
            total = total + s.a2[h * (xs - 1) + dx - 1]
        s.fin[:half] = total
        total = s.chip[base_i, half:]
        for dx in range(1, xs):
            total = total + s.b1[h * nb + (dx - 1) * ys]
        for dy in range(1, ys):
            total = total + s.b2[h * (ys - 1) + dy - 1]
        s.fin[half:] = total
        for line in range(tall):
            here = slice(line * block, (line + 1) * block)
            m = to_column(members[line : line + 1, :], square_block)
            n = to_column(s.weights[line : line + 1, :], square_block) + m
            prev = s.upper[here, h * LANES : (h + 1) * LANES]
            newup[here, h * LANES : (h + 1) * LANES] = prev + (s.fin[here, :] - m * prev) / n

    for h in range(parts):
        finish(h)

    for copy in list(asked.values()) + list(sent.values()) + list(moves.values()):
        copy.wait_send()
    for copy in list(told.values()) + list(tallied.values()) + [linked]:
        copy.wait_send()
    each(parts * chips, lambda i: pair(jnp.int32(i), 0).wait_send())
    for h in range(parts):
        give(h).wait_send()
        for name in ("diag", "dy"):
            region(name, lambda dy, dx: a1(dy, dx, h).wait_send())
        for name in ("diag", "dx"):
            region(name, lambda dy, dx: b1(dy, dx, h).wait_send())
        for dx in range(1, xs):
            a2(dx, h).wait_send()
        for dy in range(1, ys):
            b2(dy, h).wait_send()


def emit_kernel(moved_v, news_v, up_v, upnews_v, moved, news, up, upnews, sems):
    copies = [
        pltpu.make_async_copy(src, dst, sems.at[i])
        for i, (src, dst) in enumerate(((moved_v, moved), (up_v, up), (news_v, news), (upnews_v, upnews)))
    ]
    for copy in copies:
        copy.start()
    for copy in copies:
        copy.wait()


def body(
    rows_data, owner_rows, slot_rows, centroids, counts, owner_cent, slot_cent, upper, upper_counts
):
    zs, ys, xs = lax.axis_size("rows"), lax.axis_size("cx"), lax.axis_size("cy") // CORES
    chips = ys * xs
    shards = chips * CORES
    batch, features = rows_data.shape
    count, width = centroids.shape
    parts = width // LANES
    slots = upper.shape[0]
    half = slots // 2
    block = min(LANES, slots)
    capacity = -(-(2 * batch // shards) // 8) * 8
    spots = shards * capacity
    across = zs * spots // LANES
    joined = across * LANES
    tall = -(-zs // 8) * 8
    padded = -(-across // 8) * 8
    band = min(joined, 512)
    height = min(count, 512)
    na, nb = (ys - 1) * xs, (xs - 1) * ys

    vm = pl.BlockSpec(memory_space=pltpu.VMEM)
    hbm = pl.BlockSpec(memory_space=pl.ANY)
    V = pltpu.VMEM
    dma = lambda n: pltpu.SemaphoreType.DMA((n,))
    scratch = dict(
        oc=V((1, count), i32), sc=V((count // LANES, LANES), i32), cent=V((count, width), f32),
        owner=V((1, batch), i32), slot=V((1, batch), i32), rows=V((batch, features), f32),
        counts=V((count // LANES, LANES), f32), upper=V((slots, width), f32),
        weights=V((slots // block, block), f32),
        own=V((count // LANES, LANES), i32), uid=V((count // LANES, LANES), f32),
        cp=V((parts, count, 2 * LANES), bf16), oh=V((2, slots, count), bf16),
        outp=V((parts * chips, slots, LANES), f32), pair=V((parts * chips, slots, LANES), f32),
        base=V((parts * chips, slots, LANES), f32), chip=V((parts * chips, slots, LANES), f32),
        info=V((8, LANES), i32), mine=V((zs, 8, LANES), i32),
        slabs=V((parts * zs, batch, LANES), f32), pick=V((zs, spots, LANES), bf16),
        packed=V((parts * zs, spots, LANES), f32), inbox=V((parts, joined, LANES), f32),
        tags=V((tall, spots), i32), heard=V((shards, tall, spots), i32),
        ha=V((shards * 8, count), bf16), hb=V((LANES, count), bf16), hist=V((shards * 8, LANES), f32),
        hs=V((shards, 8, LANES), f32), lab=V((padded, LANES), f32), urow=V((padded, LANES), f32),
        prow=V((padded, LANES), f32), ot=V((band, count), bf16), share=V((joined, LANES), f32),
        near=V((parts, joined, LANES), f32), dl=V((parts, joined, LANES), f32),
        pd=V((parts, joined, LANES), f32), dd=V((parts, 2 * joined, 2 * LANES), bf16),
        oh3=V((slots, 2 * joined), bf16),
        a1=V((parts * na, half, LANES), f32), b1=V((parts * nb, half, LANES), f32),
        a2=V((parts * (xs - 1), half, LANES), f32), b2=V((parts * (ys - 1), half, LANES), f32),
        relay_a=V((parts * (xs - 1), half, LANES), f32), relay_b=V((parts * (ys - 1), half, LANES), f32),
        dp=V((joined, (2 * parts + 1) * LANES), bf16), oh1=V((height, joined), bf16),
        sums=V((height, (2 * parts + 1) * LANES), f32), fin=V((slots, LANES), f32),
        ld=dma(9), si=dma(zs - 1), ri=dma(zs - 1), ss=dma(parts * (zs - 1)), rs=dma(parts * (zs - 1)),
        sp=dma((shards - 1) * zs * parts), rp=dma((shards - 1) * zs * parts),
        st=dma(shards - 1), rt=dma(shards - 1), sh=dma(shards - 1), rh=dma(shards - 1),
        sb=dma(parts * chips), rb=dma(parts * chips), su=dma(1), ru=dma(1), sd=dma(parts), rd=dma(parts),
        sa1=dma(parts * na), ra1=dma(parts * na), sb1=dma(parts * nb), rb1=dma(parts * nb),
        sa2=dma(parts * (xs - 1)), ra2=dma(parts * (xs - 1)), sb2=dma(parts * (ys - 1)), rb2=dma(parts * (ys - 1)),
    )
    outs = (
        jax.ShapeDtypeStruct((count, width), f32),
        jax.ShapeDtypeStruct((count // LANES, LANES), f32),
        jax.ShapeDtypeStruct((slots, width), f32),
        jax.ShapeDtypeStruct((slots // block, block), f32),
    )
    made = pl.pallas_call(
        functools.partial(fused_kernel, tuple(scratch), (zs, ys, xs, capacity, height)),
        out_shape=outs,
        in_specs=[pl.BlockSpec(memory_space=pltpu.HBM)] * 9,
        out_specs=(vm,) * 4,
        scratch_shapes=list(scratch.values()),
        compiler_params=pltpu.CompilerParams(
            collective_id=1, has_side_effects=True, vmem_limit_bytes=44 * 1024 * 1024
        ),
        name="update",
    )(*[pltpu.with_memory_space_constraint(a, pltpu.HBM) for a in (
        rows_data, owner_rows.reshape(1, batch), slot_rows.reshape(1, batch), centroids,
        counts.reshape(-1, LANES), owner_cent.reshape(1, count), slot_cent.reshape(-1, LANES),
        upper, upper_counts.reshape(-1, block),
    )])
    moved, news, new_upper, upnews = pl.pallas_call(
        emit_kernel,
        out_shape=outs,
        in_specs=[vm] * 4,
        out_specs=(hbm,) * 4,
        scratch_shapes=[dma(4)],
        compiler_params=pltpu.CompilerParams(vmem_limit_bytes=4 * 1024 * 1024),
        name="emit",
    )(*made)
    return moved, news.reshape(-1), new_upper, upnews.reshape(-1)


def solution(mesh):
    placed = (
        P(("rows", "cx", "cy"), None),
        P(("rows", "cx", "cy"), None),
        P(("rows", "cx", "cy")),
        P(("cx", "cy"), "rows"),
        P(("cx", "cy")),
        P(("cx", "cy"), None),
        P(("cx", "cy")),
        P(("cx", "cy"), "rows"),
        P(("cx", "cy")),
    )
    return jax.shard_map(
        body,
        mesh=mesh,
        in_specs=placed,
        out_specs=(
            P(("cx", "cy"), "rows"),
            P(("cx", "cy")),
            P(("cx", "cy"), "rows"),
            P(("cx", "cy")),
        ),
        check_vma=False,
    )
```

time: 69.6 us -> 50.1 us (0.72)
  Pallas kernels: 62.6 us -> 49.1 us
  local copies, waits for them, and re-layouts: 4.55 us -> 0 us
  other arithmetic: 1.4 us -> 0 us
    pallas_call x4 -> x2, Pallas kernels: 62.6 us -> 49.1 us  [the longest x1 47.5 us: body(): pl.pallas_call(functools.partial(fused_kernel, tuple(scratch), (zs, ys, x...]
    unnamed x14 -> x0, local copies, waits for them, and re-layouts: 4.55 us -> none
    mul x1 -> x0, other arithmetic: 0.71 us -> none  [body(): ids = (owner_cent[:, 0] * upper_rows + slot_cent).reshape(-1, LANES)]
    reshape x1 -> x0, other arithmetic: 0.7 us -> none  [body(): ids = (owner_cent[:, 0] * upper_rows + slot_cent).reshape(-1, LANES)]
where the time goes in v1:
time: 50.1 us; the launch traced here: 49.9 us
  Pallas kernels  49.1 us (98%)
  between operations  0.82 us (2%)
    pallas_call x1, Pallas kernels, body(): pl.pallas_call(functools.partial(fused_kernel, tuple(scratch), (zs, ys, x...  47.5 us
    pallas_call x1, Pallas kernels, body(): pl.pallas_call(emit_kernel, out_shape=outs, in_specs=[vm] * 4, out_specs=...  1.52 us

profile of v1, /device:TPU:0, one launch (start us, length us, event | category | flops | bytes accessed | tf_op | source)
XLA Modules:
  0.0 49.9 jit_solution(18277370979658132305)
XLA Ops:
  0.6 47.5 %update.1 = (f32[2048,256]{1,0:T(8,128)S(1)}, f32[16,128]{1,0:T(8,128)S(1)}, f32[512,256]{1,0:T(8,128)S(1)}, f32[4,128]{1,0:T(4,128)S(1)}) custom-call(f32[64,1024]{1,0:T(8,128)} %rows_h.1, s32[1,64]{1,0:T(1,128)} %bitcast.12, s32[1,64]{1,0:T(1,128)} %bitcast.13, f32[2048,256]{1,0:T(8,128)} %cent_h.1, f32[16,128]{1,0:T(8,128)} %bitcast.8, ...), custom_call_target="tpu_custom_call" | custom-call | tf_op jit(solution)/shard_map/update/pallas_call | solution.py:638
  48.2 1.5 %emit.1 = (f32[2048,256]{1,0:T(8,128)}, f32[16,128]{1,0:T(8,128)}, f32[512,256]{1,0:T(8,128)}, f32[4,128]{1,0:T(4,128)}) custom-call(f32[2048,256]{1,0:T(8,128)S(1)} %get-tuple-element.12.moved_v, f32[16,128]{1,0:T(8,128)S(1)} %get-tuple-element.13.news_v, f32[512,256]{1,0:T(8,128)S(1)} %get-tuple-element.14.up_v, f32[4,128]{1,0:T(4,128)S(1)} %get-tuple-element.15.upnews_v), custom_call_target="tpu_custom_call" | custom-call | tf_op jit(solution)/shard_map/emit/pallas_call | solution.py:653

commit v2 on v1

--- a/solution.py
+++ b/solution.py
@@ -105,8 +105,8 @@
     loads = [
         pltpu.make_async_copy(src, dst, s.ld.at[i])
         for i, (src, dst) in enumerate([
-            (oc_h, s.oc), (sc_h, s.sc), (cent_h, s.cent), (owner_h, s.owner), (slot_h, s.slot),
-            (rows_h, s.rows), (counts_h, s.counts), (upper_h, s.upper), (weights_h, s.weights),
+            (owner_h, s.owner), (slot_h, s.slot), (rows_h, s.rows), (oc_h, s.oc), (sc_h, s.sc),
+            (cent_h, s.cent), (counts_h, s.counts), (upper_h, s.upper), (weights_h, s.weights),
         ])
     ]
     for copy in loads:
@@ -147,63 +147,49 @@
 
     loads[0].wait()
     loads[1].wait()
-    for b in range(lines):
-        s.own[b : b + 1, :] = s.oc[0:1, b * LANES : (b + 1) * LANES]
-    s.uid[...] = (s.own[...] * slots + s.sc[...]).astype(f32)
     loads[2].wait()
-
-    def split(b, c):
-        here = pl.ds(pl.multiple_of(b * SPAN, SPAN), SPAN)
-        for h in range(parts):
-            hi, lo = pieces(s.cent[here, h * LANES : (h + 1) * LANES])
-            s.cp[h, here, :LANES] = hi
-            s.cp[h, here, LANES:] = lo
-        return c
-
-    lax.fori_loop(0, count // SPAN, split, 0)
-
-    def pair(k, h):
-        i = h * chips + k
-        return remote(s.outp.at[i], s.pair.at[i], s.sb.at[i], s.rb.at[i], other)
-
-    def base(h, share=True):
-        def step(dy, dx):
-            k = dy * xs + dx
-            i = h * chips + k
-            for mine_too, side in ((0, 1 - core), (1, core)):
-                first = (shard_at(dy, dx, side) * slots).astype(f32)
-                one_hot(lambda b: s.uid[b : b + 1, :] - first, lines, s.oh.at[mine_too], slots)
-                total = halves(jnp.dot(s.oh[mine_too], s.cp[h], preferred_element_type=f32))
-                if mine_too:
-                    s.base[i] = total
-                else:
-                    s.outp[i] = total
-                    if share:
-                        pair(k, h).start()
-
-        return step
-
-    region("diag", base(0, False))
-
-    loads[3].wait()
-    loads[4].wait()
-    loads[5].wait()
     s.info[...] = jnp.full_like(s.info, -1)
     s.info[0:1, :batch] = s.owner[...]
     s.info[1:2, :batch] = s.slot[...]
     s.tags[...] = jnp.full_like(s.tags, count)
     pl.semaphore_wait(barrier, zs - 1 + shards - 1)
-    region("diag", lambda dy, dx: pair(dy * xs + dx, 0).start())
-
-    order = list(range(zs - 1, 0, -1))
-    asked, sent = {}, {}
-    for d in order:
-        asked[d] = started(s.info, s.mine.at[d], s.si.at[d - 1], s.ri.at[d - 1], mates[d])
-    for h in range(parts):
-        for d in order:
-            here = pl.ds(pl.multiple_of(mates[d]["rows"] * width + h * LANES, LANES), LANES)
-            i = h * (zs - 1) + d - 1
-            sent[h, d] = started(s.rows.at[:, here], s.slabs.at[h * zs + d], s.ss.at[i], s.rs.at[i], mates[d])
+
+    targets = []
+    low_end, high_end = jnp.int32(0), jnp.int32(zs - 1)
+    for _ in range(1, zs):
+        under, over = z - low_end, high_end - z
+        take = (under > over) | ((under == over) & (2 * z < zs))
+        targets.append(jnp.where(take, low_end, high_end))
+        low_end = low_end + jnp.where(take, 1, 0)
+        high_end = high_end - jnp.where(take, 0, 1)
+
+    def place_of(t):
+        if zs & (zs - 1):
+            return lax.rem(t - z + zs, zs)
+        total, bit = 0, 1
+        while bit < zs:
+            total = total + bit * lax.rem(lax.div(z, bit) + lax.div(t, bit), 2)
+            bit *= 2
+        return total
+
+    def ask(d, t):
+        return remote(s.info, s.mine.at[d], s.si.at[d - 1], s.ri.at[d - 1], {"rows": t})
+
+    def slab(d, t, h):
+        here = pl.ds(pl.multiple_of(t * width + h * LANES, LANES), LANES)
+        i = h * (zs - 1) + d - 1
+        return remote(s.rows.at[:, here], s.slabs.at[h * zs + d], s.ss.at[i], s.rs.at[i], {"rows": t})
+
+    asked = {d: ask(d, mates[d]["rows"]) for d in range(1, zs)}
+    sent = {(h, d): slab(d, mates[d]["rows"], h) for h in range(parts) for d in range(1, zs)}
+    for t in targets:
+        ask(place_of(t), t).start()
+
+    def scatter(h):
+        for t in targets:
+            slab(place_of(t), t, h).start()
+
+    scatter(0)
     s.mine[0] = s.info[...]
     for h in range(parts):
         s.slabs[h * zs] = s.rows[:, pl.ds(pl.multiple_of(z * width + h * LANES, LANES), LANES)]
@@ -241,6 +227,8 @@
         total = jnp.dot(s.pick[d, :, :batch], three, preferred_element_type=f32)
         total = (total[:, 2 * LANES :] + total[:, LANES : 2 * LANES]) + total[:, :LANES]
         s.packed[h * zs + d] = total
+
+    def post(d, h):
         for p in range(1, shards):
             t = lax.rem(me + p, shards)
             i = ((p - 1) * zs + d) * parts + h
@@ -248,6 +236,8 @@
                 s.packed.at[h * zs + d, pl.ds(pl.multiple_of(t * capacity, 8), capacity)],
                 s.inbox.at[h, pl.ds(spot(p, d), capacity)], s.sp.at[i], s.rp.at[i], peers[p],
             )
+
+    def keep(d, h):
         s.inbox[h, spot(0, d) : spot(0, d) + capacity, :] = s.packed[
             h * zs + d, pl.ds(pl.multiple_of(me * capacity, 8), capacity), :
         ]
@@ -255,7 +245,56 @@
     place(0)
     for h in range(parts):
         pack(0, h)
-
+    for h in range(parts):
+        post(0, h)
+        keep(0, h)
+
+    loads[3].wait()
+    loads[4].wait()
+    for b in range(lines):
+        s.own[b : b + 1, :] = s.oc[0:1, b * LANES : (b + 1) * LANES]
+    s.uid[...] = (s.own[...] * slots + s.sc[...]).astype(f32)
+    loads[5].wait()
+
+    def split(b, c):
+        here = pl.ds(pl.multiple_of(b * SPAN, SPAN), SPAN)
+        for h in range(parts):
+            hi, lo = pieces(s.cent[here, h * LANES : (h + 1) * LANES])
+            s.cp[h, here, :LANES] = hi
+            s.cp[h, here, LANES:] = lo
+        return c
+
+    lax.fori_loop(0, count // SPAN, split, 0)
+    loads[6].wait()
+    s.tab[...] = jnp.zeros_like(s.tab)
+    near_c, mid_c = pieces(s.counts[...])
+    far_c = (s.counts[...] - near_c.astype(f32) - mid_c.astype(f32)).astype(bf16)
+    for i, part in enumerate((near_c, mid_c, far_c) + pieces(s.uid[...])):
+        s.tab[:lines, i * LANES : (i + 1) * LANES] = part
+
+    def pair(k, h):
+        i = h * chips + k
+        return remote(s.outp.at[i], s.pair.at[i], s.sb.at[i], s.rb.at[i], other)
+
+    def base(h):
+        def step(dy, dx):
+            k = dy * xs + dx
+            i = h * chips + k
+            for mine_too, side in ((0, 1 - core), (1, core)):
+                first = (shard_at(dy, dx, side) * slots).astype(f32)
+                one_hot(lambda b: s.uid[b : b + 1, :] - first, lines, s.oh.at[mine_too], slots)
+                total = halves(jnp.dot(s.oh[mine_too], s.cp[h], preferred_element_type=f32))
+                if mine_too:
+                    s.base[i] = total
+                else:
+                    s.outp[i] = total
+            pair(k, h).start()
+
+        return step
+
+    region("diag", base(0))
+    for h in range(1, parts):
+        scatter(h)
     region("dy", base(0))
 
     for d in range(1, zs):
@@ -265,12 +304,258 @@
     told = {p: started(s.tags, s.heard.at[p], s.st.at[p - 1], s.rt.at[p - 1], peers[p]) for p in range(1, shards)}
     s.heard[0] = s.tags[...]
 
-    region("dx", base(0))
-
-    for h in range(parts):
+    def relay(h):
         for d in range(1, zs):
             sent[h, d].wait_recv()
+        for d in range(1, zs):
             pack(d, h)
+        for d in range(1, zs):
+            post(d, h)
+
+    for d in range(1, zs):
+        if d == zs - 1:
+            region("dx", base(0))
+        sent[0, d].wait_recv()
+        pack(d, 0)
+        post(d, 0)
+    for d in range(1, zs):
+        keep(d, 0)
+
+    for p in range(1, shards):
+        told[p].wait_recv()
+    few = lax.broadcasted_iota(i32, (s.tags.shape[0], LANES), 1)
+    s.lab[...] = jnp.full_like(s.lab, count)
+    for g in range(shards // per):
+        both = jnp.full(few.shape, count, i32)
+        for j in range(per):
+            turn = lax.rem((j + shards - me) * capacity, spots)
+            turned = pltpu.roll(s.heard[g * per + j], turn, 1)[:, :LANES]
+            both = jnp.where((few >= j * capacity) & (few < (j + 1) * capacity), turned, both)
+        s.lab[g * zs : (g + 1) * zs, :] = both[:zs].astype(f32)
+
+    band = s.ot.shape[0]
+
+    def fetch(jb, h):
+        here = pl.ds(pl.multiple_of(jb * band, band), band)
+        s.near[h, here, :] = halves(jnp.dot(s.ot[...], s.cp[h], preferred_element_type=f32))
+
+    across_f = lane.astype(f32)
+    across_h = across_f.astype(bf16)
+    unit, none = jnp.ones((LANES, LANES), bf16), jnp.zeros((LANES, LANES), bf16)
+
+    def gather(jb):
+        for rr in range(band // LANES):
+            r = jb * (band // LANES) + rr
+            here = pl.ds(pl.multiple_of(r * LANES, LANES), LANES)
+            row = s.lab[pl.ds(r, 1), :]
+            column = to_column(row, same)
+            top = jnp.floor(column * (1.0 / LANES))
+            label = jnp.broadcast_to(column, (LANES, LANES))
+            major = jnp.broadcast_to(top, (LANES, LANES))
+            minor = jnp.broadcast_to(column - top * float(LANES), (LANES, LANES))
+
+            def alike(q, total):
+                return total + jnp.where(label == s.lab[pl.ds(q, 1), :], 1.0, 0.0)
+
+            total = jnp.zeros((LANES, LANES), f32)
+            if across <= 8:
+                for q in range(across):
+                    total = alike(q, total)
+            else:
+                total = lax.fori_loop(0, across, alike, total)
+            line_at = jnp.where(across_f == major, 1.0, 0.0).astype(bf16)
+            found = jnp.dot(line_at, s.tab[...], preferred_element_type=f32)
+            had = (found[:, :LANES] + found[:, LANES : 2 * LANES]) + found[:, 2 * LANES : 3 * LANES]
+            named = found[:, 3 * LANES : 4 * LANES] + found[:, 4 * LANES :]
+            hit = across_f == minor
+            n = jnp.sum(jnp.where(hit, had, 0.0) + total, axis=1, keepdims=True)
+            s.share[here, :] = jnp.broadcast_to(1.0 / n, (LANES, LANES))
+            target = to_row(jnp.sum(jnp.where(hit, named, 0.0), axis=1, keepdims=True), same)
+            s.urow[pl.ds(r, 1), :] = jnp.where(row < float(count), target, -1.0)
+            spread = jnp.where(minor.astype(bf16) == across_h, unit, none)
+            major_h = major.astype(bf16)
+            for b in range(lines):
+                s.ot[rr * LANES : (rr + 1) * LANES, b * LANES : (b + 1) * LANES] = jnp.where(
+                    major_h == jnp.full((LANES, LANES), float(b), bf16), spread, none
+                )
+        for h in range(parts if joined > band else 1):
+            fetch(jb, h)
+
+    s.urow[...] = jnp.full_like(s.urow, -1.0)
+    each(joined // band, gather)
+    linked = started(s.urow, s.prow, s.su.at[0], s.ru.at[0], other)
+    ready = parts > 1
+
+    def aim(rows, begin):
+        def step(dy, dx):
+            k = (dy * xs + dx) if ready else 0
+            first = (shard_at(dy, dx, core) * slots).astype(f32)
+            one_hot(
+                lambda b: rows[b : b + 1, :] - first, across, s.oh3.at[k, :, pl.ds(begin, joined)], slots
+            )
+
+        return step
+
+    if ready:
+        for name in ("diag", "dy", "dx"):
+            region(name, aim(s.urow, 0))
+    linked.wait_recv()
+    if ready:
+        for name in ("diag", "dy", "dx"):
+            region(name, aim(s.prow, joined))
+
+    for h in range(1, parts):
+        relay(h)
+        for d in range(1, zs):
+            keep(d, h)
+
+    def give(h):
+        return remote(s.dl.at[h], s.pd.at[h], s.sd.at[h], s.rd.at[h], other)
+
+    def change(h):
+        for p in range(1, shards):
+            for d in range(zs):
+                moves[p, d, h].wait_recv()
+
+        def step(e):
+            here = pl.ds(e * SPAN, SPAN)
+            s.dl[h, here, :] = (s.inbox[h, here, :] - s.near[h, here, :]) * s.share[here, :]
+
+        each(joined // SPAN, step)
+        give(h).start()
+
+        def cut(e):
+            here = pl.ds(e * SPAN, SPAN)
+            hi, lo = pieces(s.dl[h, here, :])
+            s.dd[h, here, :LANES] = hi
+            s.dd[h, here, LANES:] = lo
+
+        each(joined // SPAN, cut)
+
+    def accept(h):
+        give(h).wait_recv()
+
+        def cut(e):
+            here = pl.ds(e * SPAN, SPAN)
+            there = pl.ds(e * SPAN + joined, SPAN)
+            hi, lo = pieces(s.pd[h, here, :])
+            s.dd[h, there, :LANES] = hi
+            s.dd[h, there, LANES:] = lo
+
+        each(joined // SPAN, cut)
+
+    def at(dy, dx):
+        return lax.rem(y + dy, ys), lax.rem(x + dx, xs)
+
+    na, nb = (ys - 1) * xs, (xs - 1) * ys
+
+    def a1(dy, dx, h):
+        i = h * na + (dy - 1) * xs + dx
+        return remote(
+            s.chip.at[h * chips + dy * xs + dx, pl.ds(0, half)], s.a1.at[i], s.sa1.at[i], s.ra1.at[i],
+            {"cx": lax.rem(y + dy, ys), "cy": cy},
+        )
+
+    def b1(dy, dx, h):
+        i = h * nb + (dx - 1) * ys + dy
+        return remote(
+            s.chip.at[h * chips + dy * xs + dx, pl.ds(half, half)], s.b1.at[i], s.sb1.at[i], s.rb1.at[i],
+            {"cx": y, "cy": lax.rem(x + dx, xs) * CORES + core},
+        )
+
+    def a2(dx, h):
+        i = h * (xs - 1) + dx - 1
+        return remote(
+            s.relay_a.at[i], s.a2.at[i], s.sa2.at[i], s.ra2.at[i],
+            {"cx": y, "cy": lax.rem(x + dx, xs) * CORES + core},
+        )
+
+    def b2(dy, h):
+        i = h * (ys - 1) + dy - 1
+        return remote(
+            s.relay_b.at[i], s.b2.at[i], s.sb2.at[i], s.rb2.at[i],
+            {"cx": lax.rem(y + dy, ys), "cy": cy},
+        )
+
+    def prepare(h):
+        def step(dy, dx):
+            k = dy * xs + dx
+            i = h * chips + k
+            o = k if ready else 0
+            if not ready:
+                aim(s.urow, 0)(dy, dx)
+                aim(s.prow, joined)(dy, dx)
+            pair(k, h).wait_recv()
+            total = halves(jnp.dot(s.oh3[o, :, :joined], s.dd[h, :joined, :], preferred_element_type=f32))
+            s.chip[i] = total + (s.base[i] + s.pair[i])
+
+        return step
+
+    def combine(h, name):
+        def step(dy, dx):
+            k = dy * xs + dx
+            i = h * chips + k
+            o = k if ready else 0
+            if not ready:
+                prepare(h)(dy, dx)
+            total = halves(jnp.dot(s.oh3[o, :, joined:], s.dd[h, joined:, :], preferred_element_type=f32))
+            s.chip[i] = s.chip[i] + total
+            if name in ("diag", "dy"):
+                a1(dy, dx, h).start()
+            if name in ("diag", "dx"):
+                b1(dy, dx, h).start()
+
+        region(name, step)
+
+    def ahead(h, names):
+        if ready:
+            for name in names:
+                region(name, prepare(h))
+
+    def forward(h):
+        for dx in range(1, xs):
+            i = h * chips + dx
+            total = s.chip[i, :half]
+            for dy in range(1, ys):
+                a1(dy, dx, h).wait_recv()
+                total = total + s.a1[h * na + (dy - 1) * xs + dx]
+            s.relay_a[h * (xs - 1) + dx - 1] = total
+            a2(dx, h).start()
+        for dy in range(1, ys):
+            i = h * chips + dy * xs
+            total = s.chip[i, half:]
+            for dx in range(1, xs):
+                b1(dy, dx, h).wait_recv()
+                total = total + s.b1[h * nb + (dx - 1) * ys + dy]
+            s.relay_b[h * (ys - 1) + dy - 1] = total
+            b2(dy, h).start()
+
+    change(0)
+    ahead(0, ("diag", "dy", "dx"))
+    accept(0)
+    for name in ("diag", "dy", "dx"):
+        combine(0, name)
+    for h in range(1, parts):
+        if joined <= band:
+            fetch(0, h)
+        region("diag", base(h))
+        region("dy", base(h))
+        region("dx", base(h))
+        if h == 1:
+            forward(0)
+        change(h)
+        ahead(h, ("diag", "dy", "dx"))
+        accept(h)
+        for name in ("diag", "dy", "dx"):
+            combine(h, name)
+    if parts == 1:
+        forward(0)
+    region("own", base(0))
+    if ready:
+        region("own", aim(s.urow, 0))
+        region("own", aim(s.prow, joined))
+    ahead(0, ("own",))
+    combine(0, "own")
 
     high = s.own[...] * 8 + lax.div(s.sc[...], block)
     low = lax.rem(s.sc[...], block)
@@ -293,178 +578,6 @@
         )
     s.hs[0] = s.hist[pl.ds(pl.multiple_of(me * 8, 8), 8), :]
 
-    loads[6].wait()
-    for p in range(1, shards):
-        told[p].wait_recv()
-    few = lax.broadcasted_iota(i32, (s.tags.shape[0], LANES), 1)
-    s.lab[...] = jnp.full_like(s.lab, count)
-    for g in range(shards // per):
-        both = jnp.full(few.shape, count, i32)
-        for j in range(per):
-            turn = lax.rem((j + shards - me) * capacity, spots)
-            turned = pltpu.roll(s.heard[g * per + j], turn, 1)[:, :LANES]
-            both = jnp.where((few >= j * capacity) & (few < (j + 1) * capacity), turned, both)
-        s.lab[g * zs : (g + 1) * zs, :] = both[:zs].astype(f32)
-
-    band = s.ot.shape[0]
-
-    def gather(jb, c):
-        for rr in range(band // LANES):
-            r = jb * (band // LANES) + rr
-            here = pl.ds(pl.multiple_of(r * LANES, LANES), LANES)
-            row = s.lab[pl.ds(r, 1), :]
-            label = jnp.broadcast_to(to_column(row, same), (LANES, LANES))
-
-            def alike(q, total):
-                return total + jnp.where(label == s.lab[pl.ds(q, 1), :], 1.0, 0.0)
-
-            mates_of = lax.fori_loop(0, across, alike, jnp.zeros((LANES, LANES), f32), unroll=min(across, 4))
-            had, named = jnp.zeros((LANES, LANES), f32), jnp.zeros((LANES, LANES), f32)
-            for b in range(lines):
-                hit = label == (lane + b * LANES).astype(f32)
-                s.ot[rr * LANES : (rr + 1) * LANES, b * LANES : (b + 1) * LANES] = jnp.where(hit, 1.0, 0.0).astype(bf16)
-                had = had + jnp.where(hit, s.counts[b : b + 1, :], 0.0)
-                named = named + jnp.where(hit, s.uid[b : b + 1, :], 0.0)
-            n = jnp.sum(had + mates_of, axis=1, keepdims=True)
-            s.share[here, :] = jnp.broadcast_to(1.0 / n, (LANES, LANES))
-            target = to_row(jnp.sum(named, axis=1, keepdims=True), same)
-            s.urow[pl.ds(r, 1), :] = jnp.where(row < float(count), target, -1.0)
-        for h in range(parts):
-            s.near[h, pl.ds(pl.multiple_of(jb * band, band), band), :] = halves(
-                jnp.dot(s.ot[...], s.cp[h], preferred_element_type=f32)
-            )
-        return c
-
-    s.urow[...] = jnp.full_like(s.urow, -1.0)
-    each(joined // band, lambda jb: gather(jb, 0))
-    linked = started(s.urow, s.prow, s.su.at[0], s.ru.at[0], other)
-
-    def give(h):
-        return remote(s.dl.at[h], s.pd.at[h], s.sd.at[h], s.rd.at[h], other)
-
-    def change(h):
-        for p in range(1, shards):
-            for d in range(zs):
-                moves[p, d, h].wait_recv()
-
-        def step(e):
-            here = pl.ds(e * SPAN, SPAN)
-            s.dl[h, here, :] = (s.inbox[h, here, :] - s.near[h, here, :]) * s.share[here, :]
-
-        each(joined // SPAN, step)
-        give(h).start()
-
-        def cut(e):
-            here = pl.ds(e * SPAN, SPAN)
-            hi, lo = pieces(s.dl[h, here, :])
-            s.dd[h, here, :LANES] = hi
-            s.dd[h, here, LANES:] = lo
-
-        each(joined // SPAN, cut)
-
-    def accept(h):
-        give(h).wait_recv()
-
-        def cut(e):
-            here = pl.ds(e * SPAN, SPAN)
-            there = pl.ds(e * SPAN + joined, SPAN)
-            hi, lo = pieces(s.pd[h, here, :])
-            s.dd[h, there, :LANES] = hi
-            s.dd[h, there, LANES:] = lo
-
-        each(joined // SPAN, cut)
-
-    def at(dy, dx):
-        return lax.rem(y + dy, ys), lax.rem(x + dx, xs)
-
-    na, nb = (ys - 1) * xs, (xs - 1) * ys
-
-    def a1(dy, dx, h):
-        i = h * na + (dy - 1) * xs + dx
-        return remote(
-            s.chip.at[h * chips + dy * xs + dx, pl.ds(0, half)], s.a1.at[i], s.sa1.at[i], s.ra1.at[i],
-            {"cx": lax.rem(y + dy, ys), "cy": cy},
-        )
-
-    def b1(dy, dx, h):
-        i = h * nb + (dx - 1) * ys + dy
-        return remote(
-            s.chip.at[h * chips + dy * xs + dx, pl.ds(half, half)], s.b1.at[i], s.sb1.at[i], s.rb1.at[i],
-            {"cx": y, "cy": lax.rem(x + dx, xs) * CORES + core},
-        )
-
-    def a2(dx, h):
-        i = h * (xs - 1) + dx - 1
-        return remote(
-            s.relay_a.at[i], s.a2.at[i], s.sa2.at[i], s.ra2.at[i],
-            {"cx": y, "cy": lax.rem(x + dx, xs) * CORES + core},
-        )
-
-    def b2(dy, h):
-        i = h * (ys - 1) + dy - 1
-        return remote(
-            s.relay_b.at[i], s.b2.at[i], s.sb2.at[i], s.rb2.at[i],
-            {"cx": lax.rem(y + dy, ys), "cy": cy},
-        )
-
-    def combine(h, name):
-        def step(dy, dx):
-            k = dy * xs + dx
-            i = h * chips + k
-            first = (shard_at(dy, dx, core) * slots).astype(f32)
-            one_hot(
-                lambda b: (s.urow[b : b + 1, :] if b < across else s.prow[b - across : b - across + 1, :]) - first,
-                2 * across, s.oh3, slots,
-            )
-            pair(k, h).wait_recv()
-            total = halves(jnp.dot(s.oh3[...], s.dd[h], preferred_element_type=f32))
-            s.chip[i] = total + (s.base[i] + s.pair[i])
-            if name in ("diag", "dy"):
-                a1(dy, dx, h).start()
-            if name in ("diag", "dx"):
-                b1(dy, dx, h).start()
-
-        region(name, step)
-
-    def forward(h):
-        for dx in range(1, xs):
-            i = h * chips + dx
-            total = s.chip[i, :half]
-            for dy in range(1, ys):
-                a1(dy, dx, h).wait_recv()
-                total = total + s.a1[h * na + (dy - 1) * xs + dx]
-            s.relay_a[h * (xs - 1) + dx - 1] = total
-            a2(dx, h).start()
-        for dy in range(1, ys):
-            i = h * chips + dy * xs
-            total = s.chip[i, half:]
-            for dx in range(1, xs):
-                b1(dy, dx, h).wait_recv()
-                total = total + s.b1[h * nb + (dx - 1) * ys + dy]
-            s.relay_b[h * (ys - 1) + dy - 1] = total
-            b2(dy, h).start()
-
-    change(0)
-    for h in range(1, parts):
-        region("diag", base(h))
-    linked.wait_recv()
-    accept(0)
-    for name in ("diag", "dy", "dx"):
-        combine(0, name)
-    for h in range(1, parts):
-        region("dy", base(h))
-        region("dx", base(h))
-        change(h)
-        if h == 1:
-            region("own", base(0))
-        accept(h)
-        for name in ("diag", "dy", "dx"):
-            combine(h, name)
-    if parts == 1:
-        region("own", base(0))
-    combine(0, "own")
-    forward(0)
-
     loads[7].wait()
     loads[8].wait()
 
@@ -500,9 +613,10 @@
     each(count // height, move)
 
     for h in range(1, parts):
+        forward(h)
         region("own", base(h))
+        ahead(h, ("own",))
         combine(h, "own")
-        forward(h)
 
     tally = s.hs[0]
     for p in range(1, shards):
@@ -613,10 +727,10 @@
         tags=V((tall, spots), i32), heard=V((shards, tall, spots), i32),
         ha=V((shards * 8, count), bf16), hb=V((LANES, count), bf16), hist=V((shards * 8, LANES), f32),
         hs=V((shards, 8, LANES), f32), lab=V((padded, LANES), f32), urow=V((padded, LANES), f32),
-        prow=V((padded, LANES), f32), ot=V((band, count), bf16), share=V((joined, LANES), f32),
+        prow=V((padded, LANES), f32), ot=V((band, count), bf16), tab=V((LANES, 5 * LANES), bf16), share=V((joined, LANES), f32),
         near=V((parts, joined, LANES), f32), dl=V((parts, joined, LANES), f32),
         pd=V((parts, joined, LANES), f32), dd=V((parts, 2 * joined, 2 * LANES), bf16),
-        oh3=V((slots, 2 * joined), bf16),
+        oh3=V((chips if parts > 1 else 1, slots, 2 * joined), bf16),
         a1=V((parts * na, half, LANES), f32), b1=V((parts * nb, half, LANES), f32),
         a2=V((parts * (xs - 1), half, LANES), f32), b2=V((parts * (ys - 1), half, LANES), f32),
         relay_a=V((parts * (xs - 1), half, LANES), f32), relay_b=V((parts * (ys - 1), half, LANES), f32),

time: 50.1 us -> 42.5 us (0.85)
  Pallas kernels: 49.1 us -> 41.5 us
    pallas_call x1, Pallas kernels: 47.5 us -> 40 us  [body(): pl.pallas_call(functools.partial(fused_kernel, tuple(scratch), (zs, ys, x...]
where the time goes in v2:
time: 42.5 us; the launch traced here: 42.3 us
  Pallas kernels  41.5 us (98%)
  between operations  0.8 us (2%)
    pallas_call x1, Pallas kernels, body(): pl.pallas_call(functools.partial(fused_kernel, tuple(scratch), (zs, ys, x...  40 us
    pallas_call x1, Pallas kernels, body(): pl.pallas_call(emit_kernel, out_shape=outs, in_specs=[vm] * 4, out_specs=...  1.52 us

profile of v2, /device:TPU:0, one launch (start us, length us, event | category | flops | bytes accessed | tf_op | source)
XLA Modules:
  0.0 42.3 jit_solution(11125512866359041217)
XLA Ops:
  0.6 40.0 %update.1 = (f32[2048,256]{1,0:T(8,128)S(1)}, f32[16,128]{1,0:T(8,128)S(1)}, f32[512,256]{1,0:T(8,128)S(1)}, f32[4,128]{1,0:T(4,128)S(1)}) custom-call(f32[64,1024]{1,0:T(8,128)} %rows_h.1, s32[1,64]{1,0:T(1,128)} %bitcast.12, s32[1,64]{1,0:T(1,128)} %bitcast.13, f32[2048,256]{1,0:T(8,128)} %cent_h.1, f32[16,128]{1,0:T(8,128)} %bitcast.8, ...), custom_call_target="tpu_custom_call" | custom-call | tf_op jit(solution)/shard_map/update/pallas_call | solution.py:752
  40.7 1.5 %emit.1 = (f32[2048,256]{1,0:T(8,128)}, f32[16,128]{1,0:T(8,128)}, f32[512,256]{1,0:T(8,128)}, f32[4,128]{1,0:T(4,128)}) custom-call(f32[2048,256]{1,0:T(8,128)S(1)} %get-tuple-element.12.moved_v, f32[16,128]{1,0:T(8,128)S(1)} %get-tuple-element.13.news_v, f32[512,256]{1,0:T(8,128)S(1)} %get-tuple-element.14.up_v, f32[4,128]{1,0:T(4,128)S(1)} %get-tuple-element.15.upnews_v), custom_call_target="tpu_custom_call" | custom-call | tf_op jit(solution)/shard_map/emit/pallas_call | solution.py:767

commit v3 on v2

--- a/solution.py
+++ b/solution.py
@@ -293,9 +293,9 @@
         return step
 
     region("diag", base(0))
+    region("dy", base(0))
     for h in range(1, parts):
         scatter(h)
-    region("dy", base(0))
 
     for d in range(1, zs):
         asked[d].wait_recv()
@@ -313,13 +313,12 @@
             post(d, h)
 
     for d in range(1, zs):
-        if d == zs - 1:
-            region("dx", base(0))
         sent[0, d].wait_recv()
         pack(d, 0)
         post(d, 0)
     for d in range(1, zs):
         keep(d, 0)
+    region("dx", base(0))
 
     for p in range(1, shards):
         told[p].wait_recv()
@@ -396,18 +395,6 @@
 
         return step
 
-    if ready:
-        for name in ("diag", "dy", "dx"):
-            region(name, aim(s.urow, 0))
-    linked.wait_recv()
-    if ready:
-        for name in ("diag", "dy", "dx"):
-            region(name, aim(s.prow, joined))
-
-    for h in range(1, parts):
-        relay(h)
-        for d in range(1, zs):
-            keep(d, h)
 
     def give(h):
         return remote(s.dl.at[h], s.pd.at[h], s.sd.at[h], s.rd.at[h], other)
@@ -531,19 +518,34 @@
             b2(dy, h).start()
 
     change(0)
-    ahead(0, ("diag", "dy", "dx"))
+    if ready:
+        region("diag", aim(s.urow, 0))
+    linked.wait_recv()
+    if ready:
+        region("diag", aim(s.prow, joined))
+    ahead(0, ("diag",))
+    for h in range(1, parts):
+        relay(h)
+        for d in range(1, zs):
+            keep(d, h)
     accept(0)
-    for name in ("diag", "dy", "dx"):
-        combine(0, name)
+    combine(0, "diag")
+    if ready:
+        for name in ("dy", "dx"):
+            region(name, aim(s.urow, 0))
+            region(name, aim(s.prow, joined))
+    ahead(0, ("dy", "dx"))
+    combine(0, "dy")
+    combine(0, "dx")
     for h in range(1, parts):
         if joined <= band:
             fetch(0, h)
         region("diag", base(h))
         region("dy", base(h))
-        region("dx", base(h))
+        change(h)
         if h == 1:
             forward(0)
-        change(h)
+        region("dx", base(h))
         ahead(h, ("diag", "dy", "dx"))
         accept(h)
         for name in ("diag", "dy", "dx"):
@@ -625,6 +627,12 @@
     members = tally[:tall, :block]
     upnews[...] = s.weights[...] + members
     square_block = square(block)
+    for line in range(tall):
+        here = slice(line * block, (line + 1) * block)
+        m = to_column(members[line : line + 1, :], square_block)
+        n = to_column(s.weights[line : line + 1, :], square_block) + m
+        s.mcol[here, :] = jnp.broadcast_to(m, (block, LANES))
+        s.ncol[here, :] = jnp.broadcast_to(1.0 / n, (block, LANES))
 
     def finish(h):
         base_i = h * chips
@@ -648,12 +656,8 @@
         for dy in range(1, ys):
             total = total + s.b2[h * (ys - 1) + dy - 1]
         s.fin[half:] = total
-        for line in range(tall):
-            here = slice(line * block, (line + 1) * block)
-            m = to_column(members[line : line + 1, :], square_block)
-            n = to_column(s.weights[line : line + 1, :], square_block) + m
-            prev = s.upper[here, h * LANES : (h + 1) * LANES]
-            newup[here, h * LANES : (h + 1) * LANES] = prev + (s.fin[here, :] - m * prev) / n
+        prev = s.upper[:, h * LANES : (h + 1) * LANES]
+        newup[:, h * LANES : (h + 1) * LANES] = prev + (s.fin[...] - s.mcol[...] * prev) * s.ncol[...]
 
     for h in range(parts):
         finish(h)
@@ -735,7 +739,7 @@
         a2=V((parts * (xs - 1), half, LANES), f32), b2=V((parts * (ys - 1), half, LANES), f32),
         relay_a=V((parts * (xs - 1), half, LANES), f32), relay_b=V((parts * (ys - 1), half, LANES), f32),
         dp=V((joined, (2 * parts + 1) * LANES), bf16), oh1=V((height, joined), bf16),
-        sums=V((height, (2 * parts + 1) * LANES), f32), fin=V((slots, LANES), f32),
+        sums=V((height, (2 * parts + 1) * LANES), f32), fin=V((slots, LANES), f32), mcol=V((slots, LANES), f32), ncol=V((slots, LANES), f32),
         ld=dma(9), si=dma(zs - 1), ri=dma(zs - 1), ss=dma(parts * (zs - 1)), rs=dma(parts * (zs - 1)),
         sp=dma((shards - 1) * zs * parts), rp=dma((shards - 1) * zs * parts),
         st=dma(shards - 1), rt=dma(shards - 1), sh=dma(shards - 1), rh=dma(shards - 1),

time: 42.5 us -> 43.3 us (1.019)
  Pallas kernels: 41.5 us -> 42.3 us
    pallas_call x1, Pallas kernels: 40 us -> 40.8 us  [body(): pl.pallas_call(functools.partial(fused_kernel, tuple(scratch), (zs, ys, x...]
where the time goes in v3:
time: 43.3 us; the launch traced here: 43.1 us
  Pallas kernels  42.3 us (98%)
  between operations  0.8 us (2%)
    pallas_call x1, Pallas kernels, body(): pl.pallas_call(functools.partial(fused_kernel, tuple(scratch), (zs, ys, x...  40.8 us
    pallas_call x1, Pallas kernels, body(): pl.pallas_call(emit_kernel, out_shape=outs, in_specs=[vm] * 4, out_specs=...  1.52 us

profile of v3, /device:TPU:0, one launch (start us, length us, event | category | flops | bytes accessed | tf_op | source)
XLA Modules:
  0.0 43.1 jit_solution(4866083560908044503)
XLA Ops:
  0.6 40.8 %update.1 = (f32[2048,256]{1,0:T(8,128)S(1)}, f32[16,128]{1,0:T(8,128)S(1)}, f32[512,256]{1,0:T(8,128)S(1)}, f32[4,128]{1,0:T(4,128)S(1)}) custom-call(f32[64,1024]{1,0:T(8,128)} %rows_h.1, s32[1,64]{1,0:T(1,128)} %bitcast.12, s32[1,64]{1,0:T(1,128)} %bitcast.13, f32[2048,256]{1,0:T(8,128)} %cent_h.1, f32[16,128]{1,0:T(8,128)} %bitcast.8, ...), custom_call_target="tpu_custom_call" | custom-call | tf_op jit(solution)/shard_map/update/pallas_call | solution.py:756
  41.5 1.5 %emit.1 = (f32[2048,256]{1,0:T(8,128)}, f32[16,128]{1,0:T(8,128)}, f32[512,256]{1,0:T(8,128)}, f32[4,128]{1,0:T(4,128)}) custom-call(f32[2048,256]{1,0:T(8,128)S(1)} %get-tuple-element.12.moved_v, f32[16,128]{1,0:T(8,128)S(1)} %get-tuple-element.13.news_v, f32[512,256]{1,0:T(8,128)S(1)} %get-tuple-element.14.up_v, f32[4,128]{1,0:T(4,128)S(1)} %get-tuple-element.15.upnews_v), custom_call_target="tpu_custom_call" | custom-call | tf_op jit(solution)/shard_map/emit/pallas_call | solution.py:771
